TPU v7x, 256 devices: a whole 4x4x8 slice. The times are simulated.
256 devices in a mesh: col: 8 (over z), row: 4 (over y), depth: 8 (over x, core).
Axes of the slice: x: 4, y: 4, z: 8, core: 2. Of those that a mesh axis runs over, the one named last changes fastest.
Arguments:
- a_mat: bfloat16 [12288, 24576], P(('depth', 'row', 'col'))
- b_mat: bfloat16 [24576, 12288], P(('depth', 'row', 'col'))
Outputs:
- output: bfloat16 [12288, 12288], P(('depth', 'row', 'col'))
All inputs are finite; a program needn't handle non-finite values.
Results may differ from a plain program's by a relative error of at most 0.001.
Values are sent between devices in bfloat16 or wider.
A program may use at most 768 MiB of HBM per device.

v0:
```python
import jax
import jax.numpy as jnp
from jax import lax
from jax.sharding import PartitionSpec as P


def solution(mesh):
    all_axes = ("depth", "row", "col")
    depth_size = mesh.shape["depth"]
    col_size = mesh.shape["col"]

    def device_block(a_rows, b_rows):
        a_part = lax.all_to_all(a_rows, "depth", 1, 0, tiled=True)
        a_block = lax.all_gather(a_part, "col", axis=0, tiled=True)
        b_part = lax.all_to_all(b_rows, "col", 1, 0, tiled=True)
        b_block = lax.all_gather(b_part, "row", axis=0, tiled=True)
        part_sum = jnp.dot(a_block, b_block, preferred_element_type=jnp.float32)
        rows_dev = a_rows.shape[0]
        n_cols = part_sum.shape[1]
        grouped = part_sum.reshape(col_size, depth_size * rows_dev, n_cols)
        summed = lax.psum_scatter(grouped, "depth", scatter_dimension=1, tiled=True)
        rounded = summed.astype(jnp.bfloat16).reshape(col_size * rows_dev, n_cols)
        return lax.all_to_all(rounded, "col", 0, 1, tiled=True)

    return jax.shard_map(device_block, mesh=mesh, in_specs=(P(all_axes, None), P(all_axes, None)), out_specs=P(all_axes, None), check_vma=False)
```

profile of v0, /device:TPU:1, one launch (start us, length us, event | category | flops | bytes accessed | tf_op | source)
XLA Modules:
  0.0 547.0 jit_solution(7006327426605926661)
XLA Ops:
  6.5 0.0 copy-start
  6.5 0.0 all-gather.5.cloned.1.call-start
  6.5 2.0 copy.16
  8.6 63.6 %all_to_all.54 = bf16[96,8,1536]{2,0,1:T(8,128)(2,1)} all-to-all(bf16[96,8,1536]{2,0,1:T(8,128)(2,1)S(1)} %bitcast.23), channel_id=1, replica_groups=mesh['col'=8,'row'=4,'depth'=8] {'col'}, dimensions={1} | all-to-all | bytes 4718592 | tf_op jit(solution)/shard_map/all_to_all | solution.py:15
  72.1 0.0 all-gather.5.cloned.1.call-update
  72.2 0.0 all-gather.3.cloned.1.call-start
  72.2 0.0 copy-done
  72.2 0.2 copy.17
  72.4 34.9 %all_to_all.55 = bf16[48,8,3072]{2,0,1:T(8,128)(2,1)} all-to-all(bf16[48,8,3072]{2,0,1:T(8,128)(2,1)S(1)} %bitcast.24), channel_id=1, replica_groups=mesh['col'=8,'row'=4,'depth'=8] {'depth'}, dimensions={1} | all-to-all | bytes 4718592 | tf_op jit(solution)/shard_map/all_to_all | solution.py:13
  107.3 0.0 all-gather.3.cloned.1.call-update
  107.3 0.0 reduce-scatter.2.cloned.1.call-start
  107.4 58.8 %all-gather.5.cloned.1.call-done = bf16[3072,1536]{1,0:T(8,128)(2,1)} async-done(((bf16[768,1536]{1,0:T(8,128)(2,1)}), bf16[3072,1536]{1,0:T(8,128)(2,1)}) %all-gather.5.cloned.1.call-update) | async-done | bytes 9437200 | tf_op jit(solution)/shard_map/all_gather | solution.py:16
  166.2 195.1 %all-gather.3.cloned.1.call-done = bf16[3072,3072]{1,0:T(8,128)(2,1)} async-done(((bf16[384,3072]{1,0:T(8,128)(2,1)}), bf16[3072,3072]{1,0:T(8,128)(2,1)}) %all-gather.3.cloned.1.call-update) | async-done | bytes 18874384 | tf_op jit(solution)/shard_map/all_gather | solution.py:14
  361.3 37.2 %fusion = f32[3072,1536]{1,0:T(8,128)} fusion(bf16[3072,3072]{1,0:T(8,128)(2,1)} %all-gather.3.cloned.1.call-done, bf16[3072,1536]{1,0:T(8,128)(2,1)} %all-gather.5.cloned.1.call-done), kind=kOutput, calls=%fused_computation.2 | convolution fusion | flops 28991029248 | bytes 47185920 | tf_op jit(solution)/shard_map/dot_general | solution.py:17
  398.5 0.0 reduce-scatter.2.cloned.1.call-update
  398.5 102.8 %reduce-scatter.2.cloned.1.call-done = f32[8,48,1536]{2,1,0:T(8,128)} async-done(((f32[8,384,1536]{2,1,0:T(8,128)}), f32[8,48,1536]{2,1,0:T(8,128)}) %reduce-scatter.2.cloned.1.call-update) | async-done | bytes 2359312 | tf_op jit(solution)/shard_map/reduce_scatter | solution.py:21
  501.3 1.8 convert_element_type.3
  503.1 36.3 %all_to_all.56 = bf16[8,48,1536]{2,1,0:T(8,128)(2,1)S(1)} all-to-all(bf16[8,48,1536]{2,1,0:T(8,128)(2,1)S(1)} %convert_element_type.3), channel_id=1, replica_groups=mesh['col'=8,'row'=4,'depth'=8] {'col'}, dimensions={0} | all-to-all | bytes 2359296 | tf_op jit(solution)/shard_map/all_to_all | solution.py:23
  539.4 1.1 copy.13
Async XLA Ops:
  6.5 65.7 %copy-start = (bf16[48,24576]{1,0:T(8,128)(2,1)S(1)}, bf16[48,24576]{1,0:T(8,128)(2,1)}, u32[]{:S(2)}) copy-start(bf16[48,24576]{1,0:T(8,128)(2,1)} %param.2) | copy-start | bytes 7077892
  6.5 159.7 %all-gather.5.cloned.1.call-start = ((), (), s32[]{:S(2)}) async-start(), calls=%async_computation.5 | async-start | bytes 11796480 | tf_op jit(solution)/shard_map/all_gather | solution.py:16
  72.2 289.1 %all-gather.3.cloned.1.call-start = ((), (), s32[]{:S(2)}) async-start(), calls=%async_computation.4 | async-start | bytes 21233664 | tf_op jit(solution)/shard_map/all_gather | solution.py:14
  107.3 394.0 %reduce-scatter.2.cloned.1.call-start = ((), (), s32[]{:S(2)}) async-start(), calls=%async_computation.6 | async-start | bytes 21233664 | tf_op jit(solution)/shard_map/reduce_scatter | solution.py:21
Sparse Core Ops, SparseCore 0:
  72.3 93.8 all-gather.4
  168.0 193.2 all-gather.2
  398.6 102.6 reduce-scatter.1
where the time goes:
time: 549 us; the launch traced here: 547 us
  waiting for transfers between devices  357 us (65%)
  blocking collectives  135 us (25%)
  matrix products  37.2 us (7%)
  between operations  13.1 us (2%)
    all_gather x1, waiting for transfers between devices, device_block(): a_block = lax.all_gather(a_part, 'col', axis=0, tiled=True)  195 us
    reduce_scatter x1, waiting for transfers between devices, device_block(): summed = lax.psum_scatter(grouped, 'depth', scatter_dimension=1, tiled=True)  103 us
    all_to_all x1, blocking collectives, device_block(): b_part = lax.all_to_all(b_rows, 'col', 1, 0, tiled=True)  63.6 us
    all_gather x1, waiting for transfers between devices, device_block(): b_block = lax.all_gather(b_part, 'row', axis=0, tiled=True)  58.8 us
    dot_general x1, matrix products, device_block(): part_sum = jnp.dot(a_block, b_block, preferred_element_type=jnp.float32)  37.2 us
    all_to_all x1, blocking collectives, device_block(): return lax.all_to_all(rounded, 'col', 0, 1, tiled=True)  36.3 us
    all_to_all x1, blocking collectives, device_block(): a_part = lax.all_to_all(a_rows, 'depth', 1, 0, tiled=True)  34.9 us
  transfers between devices with their start and end apart: 3, of which 3 were waited for; matrix products, arithmetic and copies ran while one was open for 0% of the time, Pallas kernels for 0%

commit v1 on v0

v1 whole, which is shorter than its diff:
```python
import jax
import jax.numpy as jnp
from jax import lax
from jax.experimental import pallas as pl
from jax.experimental.pallas import tpu as pltpu
from jax.sharding import PartitionSpec as P

X = 4
Y = 4
Z = 8
NC = 6
STEPS = 7
FIRST = 24
TILES = NC * Y


def kernel(a_in, b_in, out, a_buf, b_buf, c_buf, rp, rm, fp, fm, s_buf,
           zrs, zrr, zls, zlr, bs, br, axs, axr, ays, ayr, fys, fyr, ads, adr, rss, rsr, os_, or_):
    d = lax.axis_index("depth")
    y = lax.axis_index("row")
    z = lax.axis_index("col")
    x = d // 2
    c = lax.rem(d, 2)
    ra = a_in.shape[0]
    rb = b_in.shape[0]
    kx = a_in.shape[1] // X
    nd = b_in.shape[1] // (2 * Y)
    nb = nd // NC

    def rel(v, k, n):
        return lax.rem(v + k + n, n)

    def dev(dx=0, cx=0, dy=0, dz=0):
        cc = c if cx == 0 else 1 - c
        xx = x if dx == 0 else rel(x, dx, X)
        yy = y if isinstance(dy, int) and dy == 0 else rel(y, dy, Y)
        zz = z if dz == 0 else rel(z, dz, Z)
        return {"depth": 2 * xx + cc, "row": yy, "col": zz}

    def remote(src, dst, ss, rs, device):
        return pltpu.make_async_remote_copy(
            src_ref=src, dst_ref=dst, send_sem=ss, recv_sem=rs,
            device_id=device, device_id_type=pl.DeviceIdType.MESH)

    def zr(t):
        j, i = t // STEPS, lax.rem(t, STEPS)
        sh = rel(z, -(i // 2), Z)
        s = lax.rem(i, 2)
        ref = b_buf.at[j, pl.ds(4 * s, 4), pl.ds(pl.multiple_of(sh * rb, rb), rb), :]
        return remote(ref, ref, zrs.at[j, i], zrr.at[j, i], dev(dz=1))

    def zl(t):
        j, i = t // STEPS, lax.rem(t, STEPS)
        sh = rel(z, i // 2, Z)
        s = 1 - lax.rem(i, 2)
        ref = b_buf.at[j, pl.ds(4 * s, 4), pl.ds(pl.multiple_of(sh * rb, rb), rb), :]
        return remote(ref, ref, zls.at[j, i], zlr.at[j, i], dev(dz=-1))

    def bpiece(j, cx, dy):
        yy = rel(y, dy, Y)
        cc = c if cx == 0 else 1 - c
        src = b_in.at[:, pl.ds(pl.multiple_of((yy * 2 + cc) * nd + j * nb, nb), nb)]
        dst = b_buf.at[j, c * Y + y, pl.ds(pl.multiple_of(z * rb, rb), rb), :]
        m = cx * Y + dy
        if m == 0:
            return pltpu.make_async_copy(src, dst, br.at[j, 0])
        return remote(src, dst, bs.at[j, m], br.at[j, m], dev(cx=cx, dy=dy))

    BP = [(cx, dy) for dy in (2, 1, 3, 0) for cx in (0, 1)]

    def bstart(j):
        for cx, dy in BP:
            bpiece(j, cx, dy).start()

    def bwait(j):
        for cx, dy in BP:
            p = bpiece(j, cx, dy)
            if (cx, dy) == (0, 0):
                p.wait()
            else:
                p.wait_recv()

    def aslot(yr, k, cc):
        yy = rel(y, yr, Y)
        dd = 2 * rel(x, -k, X) + cc
        return a_buf.at[yy, pl.ds(pl.multiple_of(dd * ra, ra), ra), :]

    def acols(xx):
        return a_in.at[:, pl.ds(pl.multiple_of(xx * kx, kx), kx)]

    def ax(k):
        return remote(acols(rel(x, k, X)), aslot(0, 0, c), axs.at[k], axr.at[k], dev(dx=k))

    def asrc(yr, k):
        if yr == 0 and k == 0:
            return acols(x)
        return aslot(yr, k, c)

    def ay(up, k):
        return remote(asrc(0, k), aslot(0, k, c), ays.at[up, k], ayr.at[up, k], dev(dy=1 if up else -1))

    def fy(up, k):
        ref = aslot(-1 if up else 1, k, c)
        return remote(ref, ref, fys.at[up, k], fyr.at[up, k], dev(dy=1 if up else -1))

    def ad(yr, k):
        return remote(asrc(yr, k), aslot(yr, k, c), ads.at[yr, k], adr.at[yr, k], dev(cx=1))

    def aown():
        return pltpu.make_async_copy(acols(x), aslot(0, 0, c), axr.at[0])

    def crow(q, dx, cc):
        dd = 2 * rel(x, dx, X) + cc
        return c_buf.at[q, pl.ds(pl.multiple_of(dd * ra, ra), ra), :]

    def rs(q, m):
        up = m % 2 == 0
        src = (crow(q, 2, 0), crow(q, 2, 1), crow(q, 1, 1), crow(q, -1, 0), crow(q, 1, 0), crow(q, -1, 1))[m]
        dst = (rp.at[q], rm.at[q], fp.at[q, 1], fm.at[q, 0], fp.at[q, 0], fm.at[q, 1])[m]
        return remote(src, dst, rss.at[q, m], rsr.at[q, m], dev(dx=1 if up else -1))

    def ocopy(q, cx, own):
        j, yr = q // Y, lax.rem(q, Y)
        cc = c if cx == 0 else 1 - c
        dst = out.at[:, pl.ds(pl.multiple_of((2 * y + c) * nd + j * nb, nb), nb)]
        src = s_buf.at[q, cx]
        if own:
            return pltpu.make_async_copy(src, dst, os_.at[q, cx])
        return remote(src, dst, os_.at[q, cx], or_.at[q, cx], {"depth": 2 * x + cc, "row": rel(y, yr, Y), "col": z})

    peers = [dict(dx=1), dict(dx=2), dict(dx=3), dict(dz=1), dict(dz=-1)]
    peers += [dict(cx=cx, dy=dy) for cx, dy in BP if (cx, dy) != (0, 0)]
    barrier = pltpu.get_barrier_semaphore()
    for p in peers:
        pl.semaphore_signal(barrier, inc=1, device_id=dev(**p), device_id_type=pl.DeviceIdType.MESH)
    pl.semaphore_wait(barrier, len(peers))

    bstart(0)
    ax(1).start()
    ax(3).start()
    ax(2).start()
    ay(1, 0).start()
    ay(0, 0).start()
    ad(0, 0).start()
    aown().start()

    def ev_x(k):
        ax(k).wait_recv()
        ay(1, k).start()
        ay(0, k).start()
        ad(0, k).start()

    def ev_y(k):
        ay(1, k).wait_recv()
        ay(0, k).wait_recv()
        up = 1 if k in (0, 2) else 0
        fy(up, k).start()
        ad(3, k).start()
        ad(1, k).start()

    def ev_f(k):
        fy(1 if k in (0, 2) else 0, k).wait_recv()
        ad(2, k).start()

    def ev_all():
        aown().wait()
        for yr in range(Y):
            for k in range(X):
                ad(yr, k).wait_recv()

    events = [(3, ev_x, 1), (3, ev_x, 3), (6, ev_y, 0), (8, ev_x, 2), (10, ev_y, 1), (14, ev_y, 3),
              (17, ev_y, 2), (20, ev_f, 0), (20, ev_f, 1), (23, ev_f, 3), (23, ev_f, 2), (FIRST, ev_all, None)]

    def tick(t, carry):
        i = lax.rem(t, STEPS)

        @pl.when(jnp.logical_and(t >= 2, t < NC * STEPS + 2))
        def _():
            zr(t - 2).wait_recv()
            zl(t - 2).wait_recv()

        @pl.when(t < NC * STEPS)
        def _():
            @pl.when(i == 0)
            def _():
                bwait(t // STEPS)

            zr(t).start()
            zl(t).start()

            @pl.when(jnp.logical_and(i == 1, t < (NC - 1) * STEPS))
            def _():
                bstart(t // STEPS + 1)

        for when, fn, arg in events:
            @pl.when(t == when)
            def _():
                fn() if arg is None else fn(arg)

        def stage(lag, fn):
            q = t - FIRST - lag

            @pl.when(jnp.logical_and(q >= 0, q < TILES))
            def _():
                fn(q)

        def s1(q):
            for m in range(4):
                rs(q, m).start()

        def s2(q):
            rs(q, 0).wait_recv()
            rs(q, 1).wait_recv()
            u, v = crow(q, 1, 0), crow(q, -1, 1)
            u[...] = u[...] + rp[q]
            v[...] = v[...] + rm[q]

        def s2b(q):
            rs(q, 4).start()
            rs(q, 5).start()

        def s3(q):
            for m in range(2, 6):
                rs(q, m).wait_recv()
            for cx in range(2):
                cc = c if cx == 0 else 1 - c
                total = crow(q, 0, cc)[...] + fp[q, cc] + fm[q, cc]
                s_buf[q, cx] = total.astype(s_buf.dtype)

        def s4(q):
            ocopy(q, 1, False).start()

            @pl.when(lax.rem(q, Y) == 0)
            def _():
                ocopy(q, 0, True).start()

            @pl.when(lax.rem(q, Y) != 0)
            def _():
                ocopy(q, 0, False).start()

        def tile(q):
            j, yy = q // Y, rel(y, lax.rem(q, Y), Y)
            kb = b_buf.shape[2]

            def part(k):
                return jnp.dot(a_buf[yy, :, pl.ds(pl.multiple_of(k * kb, kb), kb)], b_buf[j, k],
                               preferred_element_type=jnp.float32)

            c_buf[q] = part(0)

            def add(k, carry):
                c_buf[q] = c_buf[q] + part(k)
                return carry

            lax.fori_loop(1, b_buf.shape[1], add, None)

        stage(1, s1)
        stage(4, s2b)
        stage(3, s2)
        stage(8, s4)
        stage(7, s3)
        stage(0, tile)
        return carry

    lax.fori_loop(0, FIRST + TILES + 8, tick, None)

    def zdone(t, carry):
        zr(t).wait_send()
        zl(t).wait_send()
        return carry

    lax.fori_loop(0, NC * STEPS, zdone, None)

    def bdone(j, carry):
        for cx, dy in BP:
            if (cx, dy) != (0, 0):
                bpiece(j, cx, dy).wait_send()
        return carry

    lax.fori_loop(0, NC, bdone, None)
    for k in range(X):
        if k:
            ax(k).wait_send()
        ay(1, k).wait_send()
        ay(0, k).wait_send()
        fy(1 if k in (0, 2) else 0, k).wait_send()
        for yr in range(Y):
            ad(yr, k).wait_send()

    def qdone(q, carry):
        for m in range(6):
            rs(q, m).wait_send()
        far = ocopy(q, 1, False)
        far.wait_send()
        far.wait_recv()

        @pl.when(lax.rem(q, Y) == 0)
        def _():
            ocopy(q, 0, True).wait()

        @pl.when(lax.rem(q, Y) != 0)
        def _():
            near = ocopy(q, 0, False)
            near.wait_send()
            near.wait_recv()

        return carry

    lax.fori_loop(0, TILES, qdone, None)


def solution(mesh):
    all_axes = ("depth", "row", "col")

    def device_block(a_rows, b_rows):
        ra, k = a_rows.shape
        rb, n = b_rows.shape
        nb = n // (2 * Y) // NC
        dma = pltpu.SemaphoreType.DMA
        f32, bf16 = jnp.float32, a_rows.dtype
        scratch = [
            pltpu.VMEM((Y, 2 * X * ra, k // X), bf16),
            pltpu.VMEM((NC, 2 * Y, Z * rb, nb), bf16),
            pltpu.VMEM((TILES, 2 * X * ra, nb), f32),
            pltpu.VMEM((TILES, ra, nb), f32),
            pltpu.VMEM((TILES, ra, nb), f32),
            pltpu.VMEM((TILES, 2, ra, nb), f32),
            pltpu.VMEM((TILES, 2, ra, nb), f32),
            pltpu.VMEM((TILES, 2, ra, nb), bf16),
            dma((NC, STEPS)), dma((NC, STEPS)), dma((NC, STEPS)), dma((NC, STEPS)),
            dma((NC, 2 * Y)), dma((NC, 2 * Y)),
            dma((X,)), dma((X,)), dma((2, X)), dma((2, X)), dma((2, X)), dma((2, X)),
            dma((Y, X)), dma((Y, X)),
            dma((TILES, 6)), dma((TILES, 6)), dma((TILES, 2)), dma((TILES, 2)),
        ]
        return pl.pallas_call(
            kernel,
            out_shape=jax.ShapeDtypeStruct((ra, n), bf16),
            in_specs=[pl.BlockSpec(memory_space=pl.ANY)] * 2,
            out_specs=pl.BlockSpec(memory_space=pl.ANY),
            scratch_shapes=scratch,
            compiler_params=pltpu.CompilerParams(
                collective_id=0, has_side_effects=True, vmem_limit_bytes=67043328),
        )(a_rows, b_rows)

    return jax.shard_map(device_block, mesh=mesh, in_specs=(P(all_axes, None), P(all_axes, None)),
                         out_specs=P(all_axes, None), check_vma=False)
```

time: 549 us -> 235 us (0.43)
  waiting for transfers between devices: 357 us -> 0 us
  Pallas kernels: 0 us -> 233 us
  blocking collectives: 135 us -> 0 us
  matrix products: 37.2 us -> 0 us
  between operations: 13.1 us -> 0.01 us
    all_gather x2 -> x0, waiting for transfers between devices: 254 us -> none  [the longest x1 195 us: device_block(): a_block = lax.all_gather(a_part, 'col', axis=0, tiled=True)]
    pallas_call x0 -> x1, Pallas kernels: none -> 233 us  [device_block(): pl.pallas_call(kernel, out_shape=jax.ShapeDtypeStruct((ra, n), bf16), in_...]
    all_to_all x3 -> x0, blocking collectives: 135 us -> none  [the longest x1 63.6 us: device_block(): b_part = lax.all_to_all(b_rows, 'col', 1, 0, tiled=True)]
    reduce_scatter x1 -> x0, waiting for transfers between devices: 103 us -> none  [device_block(): summed = lax.psum_scatter(grouped, 'depth', scatter_dimension=1, tiled=True)]
    dot_general x1 -> x0, matrix products: 37.2 us -> none  [device_block(): part_sum = jnp.dot(a_block, b_block, preferred_element_type=jnp.float32)]
  transfers between devices with their start and end apart: 3 -> 0, of which waited for: 3 -> 0; matrix products, arithmetic and copies ran while one was open for 0% -> 0% of each run, Pallas kernels for 0% -> 0%
where the time goes in v1:
time: 235 us
  Pallas kernels  233 us (99%)
  local copies, waits for them, and re-layouts  2.36 us (1%)
    pallas_call x1, Pallas kernels, device_block(): pl.pallas_call(kernel, out_shape=jax.ShapeDtypeStruct((ra, n), bf16), in_...  233 us

profile of v1, /device:TPU:1, one launch (start us, length us, event | category | flops | bytes accessed | tf_op | source)
XLA Modules:
  0.0 235.2 jit_solution(7715035550518995409)
XLA Ops:
  0.0 232.8 %shard_map.28 = bf16[48,12288]{1,0:T(8,128)(2,1)} custom-call(bf16[48,24576]{1,0:T(8,128)(2,1)} %a_in.1, bf16[96,12288]{1,0:T(8,128)(2,1)} %b_in.1), custom_call_target="tpu_custom_call" | custom-call | tf_op jit(solution)/shard_map/pallas_call | solution.py:336
  232.8 2.4 %copy.4 = bf16[48,12288]{1,0:T(8,128)(2,1)} copy(bf16[48,12288]{1,0:T(8,128)(2,1)} %shard_map.28) | data formatting | bytes 2359296

commit v2 on v0

v2 whole, which is shorter than its diff:
```python
import jax
import jax.numpy as jnp
from jax import lax
from jax.experimental import pallas as pl
from jax.experimental.pallas import tpu as pltpu
from jax.sharding import PartitionSpec as P

X = 4
Y = 4
Z = 8
BLOCKS = 12
PAIRS = 5
LEAD = 5
RING = LEAD + 8 * (BLOCKS // 2) + 4
FIRST = 34
PT = PAIRS * Y
ST = (BLOCKS - 2 * PAIRS) * Y


def kernel(a_in, b_in, out, a_buf, b_buf, c2, c1, rp2, rp1, rm2, rm1, fp2, fp1, fm2, fm1, s2_, s1_,
           pps, ppr, pms, pmr, zps, zpr, zms, zmr, bs, br, axs, axr, ays, ayr, fys, fyr, ads, adr,
           rss2, rsr2, rss1, rsr1, os2, or2, os1, or1):
    d = lax.axis_index("depth")
    y = lax.axis_index("row")
    z = lax.axis_index("col")
    x = d // 2
    c = lax.rem(d, 2)
    ra = a_in.shape[0]
    rb = b_in.shape[0]
    kx = a_in.shape[1] // X
    nd = b_in.shape[1] // (2 * Y)
    nb = nd // BLOCKS
    kb = Z * rb

    def rel(v, k, n):
        return lax.rem(v + k + n, n)

    def core(cx):
        return c if cx == 0 else 1 - c

    def dev(dx=0, cx=0, dy=0, dz=0):
        xx = x if isinstance(dx, int) and dx == 0 else rel(x, dx, X)
        yy = y if isinstance(dy, int) and dy == 0 else rel(y, dy, Y)
        zz = z if isinstance(dz, int) and dz == 0 else rel(z, dz, Z)
        return {"depth": 2 * xx + core(cx), "row": yy, "col": zz}

    def remote(src, dst, ss, rs, device):
        return pltpu.make_async_remote_copy(
            src_ref=src, dst_ref=dst, send_sem=ss, recv_sem=rs,
            device_id=device, device_id_type=pl.DeviceIdType.MESH)

    def own_msg(up, i):
        s = lax.rem(i, 2) if up else 1 - lax.rem(i, 2)
        sh = rel(z, -(i // 2) if up else i // 2, Z)
        half = BLOCKS // 2
        ref = b_buf.at[pl.ds(half * s, half), 0, pl.ds(pl.multiple_of(sh * rb, rb), rb), :]
        ss, rs = (pps, ppr) if up else (pms, pmr)
        return remote(ref, ref, ss.at[i], rs.at[i], dev(dz=1 if up else -1))

    def block_msg(up, blk, h, half):
        sh = rel(z, -h if up else h, Z)
        if half:
            n = rb // 2
            off = sh * rb + (0 if up else n)
        else:
            n, off = rb, sh * rb
        ref = b_buf.at[blk, pl.ds(1, 2 * Y - 1), pl.ds(pl.multiple_of(off, n), n), :]
        ss, rs = (zps, zpr) if up else (zms, zmr)
        return remote(ref, ref, ss.at[blk, h], rs.at[blk, h], dev(dz=1 if up else -1))

    def ring(t, act):
        v = t + (8 - LEAD)
        per, p = v // 8 - 1, lax.rem(v, 8)
        blk = 2 * per + lax.rem(p, 2) * (2 * (p // 4) - 1)
        h = lax.rem(p // 2 + 2 * lax.rem(p, 2), 4)
        block = jnp.logical_and(t >= LEAD, jnp.logical_and(blk >= 0, blk < BLOCKS))

        @pl.when(jnp.logical_and(t >= 0, t < LEAD))
        def _():
            for up in (True, False):
                act(own_msg(up, t))

        @pl.when(jnp.logical_and(t >= LEAD, blk < 0))
        def _():
            for up in (True, False):
                act(own_msg(up, LEAD + p // 2))

        @pl.when(jnp.logical_and(block, h < 3))
        def _():
            for up in (True, False):
                act(block_msg(up, blk, h, False))

        @pl.when(jnp.logical_and(block, h == 3))
        def _():
            for up in (True, False):
                act(block_msg(up, blk, h, True))

        return block, blk, h

    BP = [(cx, dy) for dy in (2, 1, 3, 0) for cx in (0, 1) if (cx, dy) != (0, 0)]

    def bcols(cx, dy, blk):
        yy = rel(y, dy, Y)
        return b_in.at[:, pl.ds(pl.multiple_of((yy * 2 + core(cx)) * nd + blk * nb, nb), nb)]

    def bpiece(blk, cx, dy):
        m = cx * Y + (Y - dy) % Y
        dst = b_buf.at[blk, m, pl.ds(pl.multiple_of(z * rb, rb), rb), :]
        return remote(bcols(cx, dy, blk), dst, bs.at[blk, m], br.at[blk, m], dev(cx=cx, dy=dy))

    def bown(blk):
        return pltpu.make_async_copy(
            bcols(0, 0, blk), b_buf.at[blk, 0, pl.ds(pl.multiple_of(z * rb, rb), rb), :], br.at[blk, 0])

    def bstart(blk):
        for cx, dy in BP:
            bpiece(blk, cx, dy).start()

    def bwait(blk):
        for cx, dy in BP:
            bpiece(blk, cx, dy).wait_recv()

    def aslot(yr, k, cc):
        dd = 2 * rel(x, -k, X) + cc
        return a_buf.at[rel(y, yr, Y), pl.ds(pl.multiple_of(dd * ra, ra), ra), :]

    def acols(xx):
        return a_in.at[:, pl.ds(pl.multiple_of(xx * kx, kx), kx)]

    def ax(k):
        return remote(acols(rel(x, k, X)), aslot(0, 0, c), axs.at[k], axr.at[k], dev(dx=k))

    def asrc(yr, k):
        if yr == 0 and k == 0:
            return acols(x)
        return aslot(yr, k, c)

    def ay(up, k):
        return remote(asrc(0, k), aslot(0, k, c), ays.at[up, k], ayr.at[up, k], dev(dy=1 if up else -1))

    def fy(k):
        up = k in (0, 2)
        ref = aslot(-1 if up else 1, k, c)
        return remote(ref, ref, fys.at[k], fyr.at[k], dev(dy=1 if up else -1))

    def ad(yr, k):
        return remote(asrc(yr, k), aslot(yr, k, c), ads.at[yr, k], adr.at[yr, k], dev(cx=1))

    def aown():
        return pltpu.make_async_copy(acols(x), aslot(0, 0, c), axr.at[0])

    class Tiles:
        def __init__(self, c_, rp, rm, fp, fm, s_, rss, rsr, oss, osr, first, width):
            self.c, self.rp, self.rm, self.fp, self.fm, self.s = c_, rp, rm, fp, fm, s_
            self.rss, self.rsr, self.oss, self.osr = rss, rsr, oss, osr
            self.first, self.width = first, width

        def rows(self, q, dx, cc):
            dd = 2 * rel(x, dx, X) + cc
            return self.c.at[q, pl.ds(pl.multiple_of(dd * ra, ra), ra), :]

        def part(self, q, m):
            src = (self.rows(q, 2, 0), self.rows(q, 2, 1), self.rows(q, 1, 1),
                   self.rows(q, -1, 0), self.rows(q, 1, 0), self.rows(q, -1, 1))[m]
            dst = (self.rp.at[q], self.rm.at[q], self.fp.at[q, 1],
                   self.fm.at[q, 0], self.fp.at[q, 0], self.fm.at[q, 1])[m]
            return remote(src, dst, self.rss.at[q, m], self.rsr.at[q, m], dev(dx=1 if m % 2 == 0 else -1))

        def piece(self, q, cx, own=False):
            n = nb * self.width
            col = (2 * y + c) * nd + (self.first + (q // Y) * self.width) * nb
            dst = out.at[:, pl.ds(pl.multiple_of(col, nb), n)]
            if own:
                return pltpu.make_async_copy(self.s.at[q, cx], dst, self.oss.at[q, cx])
            return remote(self.s.at[q, cx], dst, self.oss.at[q, cx], self.osr.at[q, cx],
                          dev(cx=cx, dy=lax.rem(q, Y)))

        def tile(self, q):
            blk = self.first + (q // Y) * self.width
            yy = rel(y, lax.rem(q, Y), Y)
            total = None
            for m in range(2 * Y):
                src = core(m // Y) * Y + rel(y, m % Y, Y)
                lhs = a_buf[yy, :, pl.ds(pl.multiple_of(src * kb, kb), kb)]
                rhs = [b_buf[blk + i, m] for i in range(self.width)]
                rhs = rhs[0] if self.width == 1 else jnp.concatenate(rhs, axis=1)
                part = jnp.dot(lhs, rhs, preferred_element_type=jnp.float32)
                total = part if total is None else total + part
            self.c[q] = total

        def send(self, q):
            for m in range(4):
                self.part(q, m).start()

        def relay(self, q):
            self.part(q, 0).wait_recv()
            self.part(q, 1).wait_recv()
            u, v = self.rows(q, 1, 0), self.rows(q, -1, 1)
            u[...] = u[...] + self.rp[q]
            v[...] = v[...] + self.rm[q]

        def send_relayed(self, q):
            self.part(q, 4).start()
            self.part(q, 5).start()

        def finish(self, q):
            for m in range(2, 6):
                self.part(q, m).wait_recv()
            for cx in range(2):
                cc = core(cx)
                total = self.rows(q, 0, cc)[...] + self.fp[q, cc] + self.fm[q, cc]
                self.s[q, cx] = total.astype(self.s.dtype)

        def output(self, q):
            self.piece(q, 1).start()

            @pl.when(lax.rem(q, Y) == 0)
            def _():
                self.piece(q, 0, True).start()

            @pl.when(lax.rem(q, Y) != 0)
            def _():
                self.piece(q, 0).start()

        def sent(self, q):
            for m in range(6):
                self.part(q, m).wait_send()

        def done(self, q):
            far = self.piece(q, 1)
            far.wait_send()
            far.wait_recv()

            @pl.when(lax.rem(q, Y) == 0)
            def _():
                self.piece(q, 0, True).wait()

            @pl.when(lax.rem(q, Y) != 0)
            def _():
                near = self.piece(q, 0)
                near.wait_send()
                near.wait_recv()

    two = Tiles(c2, rp2, rm2, fp2, fm2, s2_, rss2, rsr2, os2, or2, 0, 2)
    one = Tiles(c1, rp1, rm1, fp1, fm1, s1_, rss1, rsr1, os1, or1, 2 * PAIRS, 1)

    for blk in range(BLOCKS):
        bown(blk).start()
    aown().start()

    peers = [dict(dx=1), dict(dx=2), dict(dx=3), dict(dz=1), dict(dz=-1)]
    peers += [dict(cx=cx, dy=dy) for cx, dy in BP]
    barrier = pltpu.get_barrier_semaphore()
    for p in peers:
        pl.semaphore_signal(barrier, inc=1, device_id=dev(**p), device_id_type=pl.DeviceIdType.MESH)
    for blk in range(BLOCKS):
        bown(blk).wait()
    pl.semaphore_wait(barrier, len(peers))

    def a_first():
        ax(1).start()
        ax(3).start()
        ax(2).start()
        bstart(0)
        bstart(1)
        ay(1, 0).start()
        ay(0, 0).start()
        ad(0, 0).start()

    def a_x(k):
        ax(k).wait_recv()
        ay(1, k).start()
        ay(0, k).start()
        ad(0, k).start()

    def a_y(k):
        ay(1, k).wait_recv()
        ay(0, k).wait_recv()
        fy(k).start()
        ad(3, k).start()
        ad(1, k).start()

    def a_f(k):
        fy(k).wait_recv()
        ad(2, k).start()

    def a_all():
        aown().wait()
        for yr in range(Y):
            for k in range(X):
                ad(yr, k).wait_recv()

    def a_sent():
        for k in range(X):
            if k:
                ax(k).wait_send()
            ay(1, k).wait_send()
            ay(0, k).wait_send()
            fy(k).wait_send()
            for yr in range(Y):
                ad(yr, k).wait_send()

    def b_sent():
        def body(blk, carry):
            for cx, dy in BP:
                bpiece(blk, cx, dy).wait_send()
            return carry

        lax.fori_loop(0, BLOCKS, body, None)

    events = [(0, a_first, ()), (5, a_x, (1,)), (5, a_x, (3,)), (12, a_x, (2,)), (13, a_y, (0,)), (13, a_y, (1,)),
              (17, a_y, (3,)), (21, a_y, (2,)), (31, a_f, (0,)), (31, a_f, (1,)), (33, a_f, (3,)), (33, a_f, (2,)),
              (FIRST, a_all, ()), (42, a_sent, ()), (46, b_sent, ())]

    def tick(t, carry):
        ring(t - 2, lambda m: m.wait_recv())
        v = t + (8 - LEAD)
        per, p = v // 8 - 1, lax.rem(v, 8)
        live = jnp.logical_and(t >= LEAD, per < BLOCKS // 2)

        @pl.when(jnp.logical_and(live, p == 0))
        def _():
            bwait(2 * per)

        @pl.when(jnp.logical_and(live, p == 5))
        def _():
            bwait(2 * per + 1)

        ring(t, lambda m: m.start())

        @pl.when(jnp.logical_and(p == 7, per < BLOCKS // 2 - 2))
        def _():
            bstart(2 * per + 4)
            bstart(2 * per + 5)

        for when, fn, arg in events:
            @pl.when(t == when)
            def _():
                fn(*arg)

        ring(t - 8, lambda m: m.wait_send())

        def stage(lag, name):
            u = t - FIRST - lag

            @pl.when(jnp.logical_and(u >= 0, u < PT))
            def _():
                getattr(two, name)(u)

            @pl.when(jnp.logical_and(u >= PT, u < PT + ST))
            def _():
                getattr(one, name)(u - PT)

        stage(1, "send")
        stage(4, "send_relayed")
        stage(7, "output")
        stage(3, "relay")
        stage(6, "finish")
        stage(0, "tile")
        stage(9, "sent")
        stage(10, "done")
        return carry

    lax.fori_loop(0, FIRST + PT + ST + 10, tick, None)


def solution(mesh):
    all_axes = ("depth", "row", "col")

    def device_block(a_rows, b_rows):
        ra, k = a_rows.shape
        rb, n = b_rows.shape
        nb = n // (2 * Y) // BLOCKS
        dma = pltpu.SemaphoreType.DMA
        f32, bf16 = jnp.float32, a_rows.dtype

        def both(*tail, dtype):
            return [pltpu.VMEM((PT, *tail, 2 * nb), dtype), pltpu.VMEM((ST, *tail, nb), dtype)]

        scratch = [
            pltpu.VMEM((Y, 2 * X * ra, k // X), bf16),
            pltpu.VMEM((BLOCKS, 2 * Y, Z * rb, nb), bf16),
            *both(2 * X * ra, dtype=f32),
            *both(ra, dtype=f32), *both(ra, dtype=f32),
            *both(2, ra, dtype=f32), *both(2, ra, dtype=f32),
            *both(2, ra, dtype=bf16),
            dma((7,)), dma((7,)), dma((7,)), dma((7,)),
            dma((BLOCKS, 4)), dma((BLOCKS, 4)), dma((BLOCKS, 4)), dma((BLOCKS, 4)),
            dma((BLOCKS, 2 * Y)), dma((BLOCKS, 2 * Y)),
            dma((X,)), dma((X,)), dma((2, X)), dma((2, X)), dma((X,)), dma((X,)),
            dma((Y, X)), dma((Y, X)),
            dma((PT, 6)), dma((PT, 6)), dma((ST, 6)), dma((ST, 6)),
            dma((PT, 2)), dma((PT, 2)), dma((ST, 2)), dma((ST, 2)),
        ]
        return pl.pallas_call(
            kernel,
            out_shape=jax.ShapeDtypeStruct((ra, n), bf16),
            in_specs=[pl.BlockSpec(memory_space=pl.ANY)] * 2,
            out_specs=pl.BlockSpec(memory_space=pl.ANY),
            scratch_shapes=scratch,
            compiler_params=pltpu.CompilerParams(
                collective_id=0, has_side_effects=True, vmem_limit_bytes=67043328),
        )(a_rows, b_rows)

    return jax.shard_map(device_block, mesh=mesh, in_specs=(P(all_axes, None), P(all_axes, None)),
                         out_specs=P(all_axes, None), check_vma=False)
```

time: 549 us -> 232 us (0.42)
  waiting for transfers between devices: 357 us -> 0 us
  Pallas kernels: 0 us -> 230 us
  blocking collectives: 135 us -> 0 us
  matrix products: 37.2 us -> 0 us
  between operations: 13.1 us -> 0.01 us
    all_gather x2 -> x0, waiting for transfers between devices: 254 us -> none  [the longest x1 195 us: device_block(): a_block = lax.all_gather(a_part, 'col', axis=0, tiled=True)]
    pallas_call x0 -> x1, Pallas kernels: none -> 230 us  [device_block(): pl.pallas_call(kernel, out_shape=jax.ShapeDtypeStruct((ra, n), bf16), in_...]
    all_to_all x3 -> x0, blocking collectives: 135 us -> none  [the longest x1 63.6 us: device_block(): b_part = lax.all_to_all(b_rows, 'col', 1, 0, tiled=True)]
    reduce_scatter x1 -> x0, waiting for transfers between devices: 103 us -> none  [device_block(): summed = lax.psum_scatter(grouped, 'depth', scatter_dimension=1, tiled=True)]
    dot_general x1 -> x0, matrix products: 37.2 us -> none  [device_block(): part_sum = jnp.dot(a_block, b_block, preferred_element_type=jnp.float32)]
  transfers between devices with their start and end apart: 3 -> 0, of which waited for: 3 -> 0; matrix products, arithmetic and copies ran while one was open for 0% -> 0% of each run, Pallas kernels for 0% -> 0%
where the time goes in v2:
time: 232 us
  Pallas kernels  230 us (99%)
  local copies, waits for them, and re-layouts  2.36 us (1%)
    pallas_call x1, Pallas kernels, device_block(): pl.pallas_call(kernel, out_shape=jax.ShapeDtypeStruct((ra, n), bf16), in_...  230 us

profile of v2, /device:TPU:1, one launch (start us, length us, event | category | flops | bytes accessed | tf_op | source)
XLA Modules:
  0.0 232.1 jit_solution(1976396024296664400)
XLA Ops:
  0.0 229.7 %shard_map.28 = bf16[48,12288]{1,0:T(8,128)(2,1)} custom-call(bf16[48,24576]{1,0:T(8,128)(2,1)} %a_in.1, bf16[96,12288]{1,0:T(8,128)(2,1)} %b_in.1), custom_call_target="tpu_custom_call" | custom-call | tf_op jit(solution)/shard_map/pallas_call | solution.py:395
  229.7 2.4 %copy.4 = bf16[48,12288]{1,0:T(8,128)(2,1)} copy(bf16[48,12288]{1,0:T(8,128)(2,1)} %shard_map.28) | data formatting | bytes 2359296

commit v3 on v2

v3 whole, which is shorter than its diff:
```python
import jax
import jax.numpy as jnp
from jax import lax
from jax.experimental import pallas as pl
from jax.experimental.pallas import tpu as pltpu
from jax.sharding import PartitionSpec as P

X = 4
Y = 4
Z = 8
BLOCKS = 12
PAIRS = 4
LEAD = 6
END = 43
FIRST = 21
SINGLE = 34
PT = PAIRS * Y
ST = (BLOCKS - 2 * PAIRS) * Y


def kernel(a_in, b_in, out, a_buf, b_buf, c2, c1, rp2, rp1, rm2, rm1, fp2, fp1, fm2, fm1, s2_, s1_,
           zps, zpr, zms, zmr, bs, br, bo, axr, ayr, fyr, adr, as24, as7,
           rss2, rsr2, rsf2, oss2, osr2, oso2, rss1, rsr1, rsf1, oss1, osr1, oso1):
    d = lax.axis_index("depth")
    y = lax.axis_index("row")
    z = lax.axis_index("col")
    x = d // 2
    c = lax.rem(d, 2)
    ra = a_in.shape[0]
    rb = b_in.shape[0]
    kx = a_in.shape[1] // X
    nd = b_in.shape[1] // (2 * Y)
    nb = nd // BLOCKS
    kb = Z * rb

    def rel(v, k, n):
        return lax.rem(v + k + n, n)

    def core(cx):
        return c if cx == 0 else 1 - c

    def dev(dx=0, cx=0, dy=0, dz=0):
        xx = x if isinstance(dx, int) and dx == 0 else rel(x, dx, X)
        yy = y if isinstance(dy, int) and dy == 0 else rel(y, dy, Y)
        zz = z if isinstance(dz, int) and dz == 0 else rel(z, dz, Z)
        return {"depth": 2 * xx + core(cx), "row": yy, "col": zz}

    def remote(src, dst, ss, rs, device):
        return pltpu.make_async_remote_copy(
            src_ref=src, dst_ref=dst, send_sem=ss, recv_sem=rs,
            device_id=device, device_id_type=pl.DeviceIdType.MESH)

    def landed(ref, sem):
        remote(ref, ref, bs, sem, dev(dz=1)).wait_recv()

    def left(ref, sem):
        remote(ref, ref, sem, bo, dev(dz=1)).wait_send()

    def sems(up, kind, t):
        ss, rs = (zps, zpr) if up else (zms, zmr)
        return ss.at[kind, lax.rem(t, 4)], rs.at[kind, lax.rem(t, 4)]

    def own_msg(up, i, t):
        s = lax.rem(i, 2) if up else 1 - lax.rem(i, 2)
        sh = rel(z, -(i // 2) if up else i // 2, Z)
        half = BLOCKS // 2
        ref = b_buf.at[pl.ds(half * s, half), 0, pl.ds(pl.multiple_of(sh * rb, rb), rb), :]
        return remote(ref, ref, *sems(up, 0, t), dev(dz=1 if up else -1))

    def block_msg(up, blk, h, half, t):
        sh = rel(z, -h if up else h, Z)
        if half:
            n = rb // 2
            off = sh * rb + (0 if up else n)
        else:
            n, off = rb, sh * rb
        ref = b_buf.at[blk, pl.ds(1, 2 * Y - 1), pl.ds(pl.multiple_of(off, n), n), :]
        return remote(ref, ref, *sems(up, 1 if half else 0, t), dev(dz=1 if up else -1))

    def last_msg(up, h, i):
        sh = rel(z, -h if up else h, Z)
        n = rb // 2
        off = sh * rb + n * (i if up else 1 - i)
        ref = b_buf.at[BLOCKS - 1, pl.ds(1, 2 * Y - 1), pl.ds(pl.multiple_of(off, n), n), :]
        return remote(ref, ref, *sems(up, i, END - 4 + 2 * h), dev(dz=1 if up else -1))

    def ring(t, act):
        u = t - LEAD
        odd = lax.rem(u, 2)
        k = (u + 3 * odd) // 2
        blk, h = 2 * (k // 3) - odd, lax.rem(k, 3)
        block = (t >= LEAD) & (blk >= 0)

        @pl.when((t >= 0) & ((t < LEAD) | (blk < 0)))
        def _():
            for up in (True, False):
                act(own_msg(up, t - t // (LEAD + 1), t))

        @pl.when(block & (h == 0) & (blk >= 2))
        def _():
            for up in (True, False):
                act(block_msg(up, blk - 2, 3, True, t))

        @pl.when(block & (3 * blk + h <= 3 * (BLOCKS - 1)))
        def _():
            for up in (True, False):
                act(block_msg(up, blk, h, False, t))

    BP = [(cx, dy) for dy in (2, 1, 3, 0) for cx in (0, 1) if (cx, dy) != (0, 0)]

    def bcols(cx, dy, blk):
        yy = rel(y, dy, Y)
        return b_in.at[:, pl.ds(pl.multiple_of((yy * 2 + core(cx)) * nd + blk * nb, nb), nb)]

    def bpiece(blk, cx, dy):
        m = cx * Y + (Y - dy) % Y
        dst = b_buf.at[blk, m, pl.ds(pl.multiple_of(z * rb, rb), rb), :]
        return remote(bcols(cx, dy, blk), dst, bs, br.at[blk], dev(cx=cx, dy=dy))

    def bown(blk):
        return pltpu.make_async_copy(
            bcols(0, 0, blk), b_buf.at[blk, 0, pl.ds(pl.multiple_of(z * rb, rb), rb), :], bo)

    def bstart(blk):
        for cx, dy in BP:
            bpiece(blk, cx, dy).start()

    def bwait(blk):
        landed(b_buf.at[blk, pl.ds(1, 2 * Y - 1), pl.ds(pl.multiple_of(z * rb, rb), rb), :], br.at[blk])

    def aslot(yr, k, cc):
        dd = 2 * rel(x, -k, X) + cc
        return a_buf.at[rel(y, yr, Y), pl.ds(pl.multiple_of(dd * ra, ra), ra), :]

    def acols(xx):
        return a_in.at[:, pl.ds(pl.multiple_of(xx * kx, kx), kx)]

    def ax(k):
        return remote(acols(rel(x, k, X)), aslot(0, 0, c), as7, axr.at[k], dev(dx=k))

    def asrc(yr, k):
        if yr == 0 and k == 0:
            return acols(x)
        return aslot(yr, k, c)

    def ay(up, k):
        return remote(asrc(0, k), aslot(0, k, c), as24, ayr.at[up, k], dev(dy=1 if up else -1))

    def fy(k):
        up = k in (0, 2)
        ref = aslot(-1 if up else 1, k, c)
        return remote(ref, ref, as7, fyr.at[k], dev(dy=1 if up else -1))

    def ad(yr, k):
        return remote(asrc(yr, k), aslot(yr, k, c), as24, adr.at[yr], dev(cx=1))

    def aown():
        return pltpu.make_async_copy(acols(x), aslot(0, 0, c), axr.at[0])

    class Tiles:
        def __init__(self, c_, rp, rm, fp, fm, s_, rss, rsr, rsf, oss, osr, oso, first, width):
            self.c, self.rp, self.rm, self.fp, self.fm, self.s = c_, rp, rm, fp, fm, s_
            self.rss, self.rsr, self.rsf, self.oss, self.osr, self.oso = rss, rsr, rsf, oss, osr, oso
            self.first, self.width = first, width

        def rows(self, q, dx, cc):
            dd = 2 * rel(x, dx, X) + cc
            return self.c.at[q, pl.ds(pl.multiple_of(dd * ra, ra), ra), :]

        def part(self, q, m):
            src = (self.rows(q, 2, 0), self.rows(q, 2, 1), self.rows(q, 1, 1),
                   self.rows(q, -1, 0), self.rows(q, 1, 0), self.rows(q, -1, 1))[m]
            dst = (self.rp.at[q], self.rm.at[q], self.fp.at[q, 1],
                   self.fm.at[q, 0], self.fp.at[q, 0], self.fm.at[q, 1])[m]
            return remote(src, dst, self.rss, (self.rsr if m < 2 else self.rsf).at[q], dev(dx=1 if m % 2 == 0 else -1))

        def piece(self, q, cx, own=False):
            n = nb * self.width
            col = (2 * y + c) * nd + (self.first + (q // Y) * self.width) * nb
            dst = out.at[:, pl.ds(pl.multiple_of(col, nb), n)]
            if own:
                return pltpu.make_async_copy(self.s.at[q, cx], dst, self.oso)
            return remote(self.s.at[q, cx], dst, self.oss, self.osr, dev(cx=cx, dy=lax.rem(q, Y)))

        def tile(self, q):
            blk = self.first + (q // Y) * self.width
            yy = rel(y, lax.rem(q, Y), Y)
            total = None
            for m in range(2 * Y):
                src = core(m // Y) * Y + rel(y, m % Y, Y)
                lhs = a_buf[yy, :, pl.ds(pl.multiple_of(src * kb, kb), kb)]
                rhs = [b_buf[blk + i, m] for i in range(self.width)]
                rhs = rhs[0] if self.width == 1 else jnp.concatenate(rhs, axis=1)
                part = jnp.dot(lhs, rhs, preferred_element_type=jnp.float32)
                total = part if total is None else total + part
            self.c[q] = total

        def send(self, q):
            for m in range(4):
                self.part(q, m).start()

        def relay(self, q):
            landed(self.c.at[q, pl.ds(0, 2 * ra), :], self.rsr.at[q])
            u, v = self.rows(q, 1, 0), self.rows(q, -1, 1)
            u[...] = u[...] + self.rp[q]
            v[...] = v[...] + self.rm[q]

        def send_relayed(self, q):
            self.part(q, 4).start()
            self.part(q, 5).start()

        def finish(self, q):
            landed(self.c.at[q, pl.ds(0, 4 * ra), :], self.rsf.at[q])
            for cx in range(2):
                cc = core(cx)
                total = self.rows(q, 0, cc)[...] + self.fp[q, cc] + self.fm[q, cc]
                self.s[q, cx] = total.astype(self.s.dtype)

        def output(self, q):
            self.piece(q, 1).start()

            @pl.when(lax.rem(q, Y) == 0)
            def _():
                self.piece(q, 0, True).start()

            @pl.when(lax.rem(q, Y) != 0)
            def _():
                self.piece(q, 0).start()

        def end(self, tiles):
            left(self.c.at[pl.ds(0, tiles * 6 // (2 * X)), :, :], self.rss)
            left(self.s.at[pl.ds(0, tiles * 7 // 8)], self.oss)
            landed(self.s.at[pl.ds(0, tiles // 8)], self.oso)
            landed(self.s.at[pl.ds(0, tiles * 7 // 8)], self.osr)

    two = Tiles(c2, rp2, rm2, fp2, fm2, s2_, rss2, rsr2, rsf2, oss2, osr2, oso2, 0, 2)
    one = Tiles(c1, rp1, rm1, fp1, fm1, s1_, rss1, rsr1, rsf1, oss1, osr1, oso1, 2 * PAIRS, 1)

    for blk in range(BLOCKS):
        bown(blk).start()
    aown().start()

    peers = [dict(dx=1), dict(dx=2), dict(dx=3), dict(dz=1), dict(dz=-1)]
    peers += [dict(cx=cx, dy=dy) for cx, dy in BP]
    barrier = pltpu.get_barrier_semaphore()
    for p in peers:
        pl.semaphore_signal(barrier, inc=1, device_id=dev(**p), device_id_type=pl.DeviceIdType.MESH)
    landed(b_buf.at[:, 0, pl.ds(pl.multiple_of(z * rb, rb), rb), :], bo)
    pl.semaphore_wait(barrier, len(peers))

    def a_first():
        ax(1).start()
        ax(3).start()
        ax(2).start()
        bstart(0)
        bstart(1)
        ay(1, 0).start()
        ay(0, 0).start()
        ad(0, 0).start()

    def a_x(k):
        ax(k).wait_recv()
        ay(1, k).start()
        ay(0, k).start()
        ad(0, k).start()

    def a_y(k):
        ay(1, k).wait_recv()
        ay(0, k).wait_recv()
        fy(k).start()
        ad(3, k).start()
        ad(1, k).start()

    def a_f(k):
        fy(k).wait_recv()
        ad(2, k).start()

    def a_rows(yr):
        if yr == 0:
            aown().wait()
        landed(a_buf.at[0, pl.ds(0, X * ra), :], adr.at[yr])

    def start(m):
        m.start()

    def recv(m):
        m.wait_recv()

    def sent(m):
        m.wait_send()

    def last_hop(h, i, act):
        for up in (True, False):
            act(last_msg(up, h, i))

    def run(t, group):
        for at, calls in group.items():
            @pl.when(t == at)
            def _():
                for fn, *arg in calls:
                    fn(*arg)

    ahead = {0: [(a_first,)], 5: [(a_x, 1), (a_x, 3)], 12: [(a_x, 2), (a_y, 0), (a_y, 1)], 14: [(a_y, 3)],
             18: [(a_y, 2)]}
    beside = {FIRST: [(a_rows, 0), (a_rows, 1), (a_rows, 3)], 26: [(a_f, 0), (a_f, 1)], 29: [(a_f, 3), (a_f, 2)],
              FIRST + 10: [(a_rows, 2)]}
    tail = {44: [(last_hop, 1, 0, recv), (last_hop, 2, 0, start), (last_hop, 1, 1, recv), (last_hop, 2, 1, start)],
            47: [(last_hop, 2, 0, recv), (last_hop, 1, 0, sent), (last_hop, 3, 0, start)],
            50: [(last_hop, 2, 1, recv), (last_hop, 1, 1, sent)], 52: [(last_hop, 3, 0, recv)]}
    last_slot = SINGLE + 6 * (BLOCKS - 2 * PAIRS - 1) + Y - 1

    def pair_stage(slot, name, lag):
        w = slot - lag
        i, r = w // 4, lax.rem(w, 4)
        late, last = i // 5, i // 7
        q = (1 - late) * (Y * (i - 2 * (i // 4)) + r + r // 2) + (late - last) * (Y * r + 2) + last * (12 + r)
        some = (r < 3) & ((i < 2) | (i == 4) | (i == 5))

        @pl.when((w >= 0) & (w < 32) & (some | (i == 7)))
        def _():
            getattr(two, name)(q)

    def block_stage(slot, name, lag):
        v = slot - SINGLE - lag
        k, r = v // 6, lax.rem(v, 6)

        @pl.when((v >= 0) & (k < BLOCKS - 2 * PAIRS) & (r < Y))
        def _():
            getattr(one, name)(Y * k + r)

    def slots(slot, carry):
        @pl.when(slot < 32 + 16)
        def _():
            pair_stage(slot, "send", 1)
            pair_stage(slot, "send_relayed", 7)
            pair_stage(slot, "output", 15)
            pair_stage(slot, "relay", 6)
            pair_stage(slot, "finish", 14)
            pair_stage(slot, "tile", 0)

        @pl.when(slot >= SINGLE)
        def _():
            block_stage(slot, "send", 1)

            @pl.when((slot >= 44) & (slot <= 52))
            def _():
                run(slot, tail)

            block_stage(slot, "send_relayed", 5)
            block_stage(slot, "output", 10)
            block_stage(slot, "tile", 0)
            block_stage(slot, "relay", 4)
            block_stage(slot, "finish", 9)

        return carry

    def tick(t, carry):
        @pl.when(t < END + 2)
        def _():
            ring(t - 2, recv)
            ring(t - 4, sent)
            ahead3 = lax.rem(t, 3)

            @pl.when((ahead3 == 0) & (t >= LEAD) & (t < LEAD + 3 * BLOCKS))
            def _():
                bwait((t - LEAD) // 3)

            @pl.when(t < END)
            def _():
                ring(t, start)

            @pl.when(t == END - 2)
            def _():
                last_hop(1, 0, start)
                last_hop(1, 1, start)

            @pl.when((ahead3 == 1) & (t >= 4) & (t < 3 * BLOCKS - 2))
            def _():
                bstart((t + 2) // 3)

            @pl.when(t < FIRST)
            def _():
                run(t, ahead)

            @pl.when(t >= FIRST)
            def _():
                run(t, beside)

        @pl.when(t >= FIRST)
        def _():
            first = 2 * (t - FIRST)
            lax.fori_loop(first, first + 2, slots, None)

        return carry

    lax.fori_loop(0, FIRST + (last_slot + 10) // 2 + 1, tick, None)

    def ring_sent(t, carry):
        ring(t, sent)
        return carry

    lax.fori_loop(END - 1, END, ring_sent, None)
    for h, i in ((2, 0), (2, 1), (3, 0)):
        last_hop(h, i, sent)
    left(b_buf.at[:, pl.ds(1, 2 * Y - 1), pl.ds(0, rb), :], bs)
    left(a_buf.at[pl.ds(0, 3)], as24)
    left(a_buf.at[0, pl.ds(0, 7 * ra), :], as7)
    two.end(PT)
    one.end(ST)


def solution(mesh):
    all_axes = ("depth", "row", "col")

    def device_block(a_rows, b_rows):
        ra, k = a_rows.shape
        rb, n = b_rows.shape
        nb = n // (2 * Y) // BLOCKS
        dma = pltpu.SemaphoreType.DMA
        f32, bf16 = jnp.float32, a_rows.dtype

        def both(*tail, dtype):
            return [pltpu.VMEM((PT, *tail, 2 * nb), dtype), pltpu.VMEM((ST, *tail, nb), dtype)]

        scratch = [
            pltpu.VMEM((Y, 2 * X * ra, k // X), bf16),
            pltpu.VMEM((BLOCKS, 2 * Y, Z * rb, nb), bf16),
            *both(2 * X * ra, dtype=f32),
            *both(ra, dtype=f32), *both(ra, dtype=f32),
            *both(2, ra, dtype=f32), *both(2, ra, dtype=f32),
            *both(2, ra, dtype=bf16),
            dma((2, 4)), dma((2, 4)), dma((2, 4)), dma((2, 4)),
            dma, dma((BLOCKS,)), dma, dma((X,)), dma((2, X)), dma((X,)), dma((Y,)), dma, dma,
            dma, dma((PT,)), dma((PT,)), dma, dma, dma,
            dma, dma((ST,)), dma((ST,)), dma, dma, dma,
        ]
        return pl.pallas_call(
            kernel,
            out_shape=jax.ShapeDtypeStruct((ra, n), bf16),
            in_specs=[pl.BlockSpec(memory_space=pl.ANY)] * 2,
            out_specs=pl.BlockSpec(memory_space=pl.ANY),
            scratch_shapes=scratch,
            compiler_params=pltpu.CompilerParams(
                collective_id=0, has_side_effects=True, vmem_limit_bytes=67043328),
        )(a_rows, b_rows)

    return jax.shard_map(device_block, mesh=mesh, in_specs=(P(all_axes, None), P(all_axes, None)),
                         out_specs=P(all_axes, None), check_vma=False)
```

time: 232 us -> 217 us (0.935)
  Pallas kernels: 230 us -> 215 us
    pallas_call x1, Pallas kernels: 230 us -> 215 us  [device_block(): pl.pallas_call(kernel, out_shape=jax.ShapeDtypeStruct((ra, n), bf16), in_...]
where the time goes in v3:
time: 217 us
  Pallas kernels  215 us (99%)
  local copies, waits for them, and re-layouts  2.36 us (1%)
    pallas_call x1, Pallas kernels, device_block(): pl.pallas_call(kernel, out_shape=jax.ShapeDtypeStruct((ra, n), bf16), in_...  215 us

profile of v3, /device:TPU:1, one launch (start us, length us, event | category | flops | bytes accessed | tf_op | source)
XLA Modules:
  0.0 217.3 jit_solution(4770601715187089281)
XLA Ops:
  0.0 214.9 %shard_map.28 = bf16[48,12288]{1,0:T(8,128)(2,1)} custom-call(bf16[48,24576]{1,0:T(8,128)(2,1)} %a_in.1, bf16[96,12288]{1,0:T(8,128)(2,1)} %b_in.1), custom_call_target="tpu_custom_call" | custom-call | tf_op jit(solution)/shard_map/pallas_call | solution.py:437
  214.9 2.4 %copy.4 = bf16[48,12288]{1,0:T(8,128)(2,1)} copy(bf16[48,12288]{1,0:T(8,128)(2,1)} %shard_map.28) | data formatting | bytes 2359296

commit v4 on v3

--- a/solution.py
+++ b/solution.py
@@ -12,15 +12,15 @@
 PAIRS = 4
 LEAD = 6
 END = 43
-FIRST = 21
-SINGLE = 34
+FIRST = 22
+SINGLE = 32
 PT = PAIRS * Y
 ST = (BLOCKS - 2 * PAIRS) * Y
 
 
 def kernel(a_in, b_in, out, a_buf, b_buf, c2, c1, rp2, rp1, rm2, rm1, fp2, fp1, fm2, fm1, s2_, s1_,
            zps, zpr, zms, zmr, bs, br, bo, axr, ayr, fyr, adr, as24, as7,
-           rss2, rsr2, rsf2, oss2, osr2, oso2, rss1, rsr1, rsf1, oss1, osr1, oso1):
+           rss2, rsr2, rsf2, oss2, osr2, rss1, rsr1, rsf1, oss1, osr1):
     d = lax.axis_index("depth")
     y = lax.axis_index("row")
     z = lax.axis_index("col")
@@ -158,9 +158,9 @@
         return pltpu.make_async_copy(acols(x), aslot(0, 0, c), axr.at[0])
 
     class Tiles:
-        def __init__(self, c_, rp, rm, fp, fm, s_, rss, rsr, rsf, oss, osr, oso, first, width):
+        def __init__(self, c_, rp, rm, fp, fm, s_, rss, rsr, rsf, oss, osr, first, width):
             self.c, self.rp, self.rm, self.fp, self.fm, self.s = c_, rp, rm, fp, fm, s_
-            self.rss, self.rsr, self.rsf, self.oss, self.osr, self.oso = rss, rsr, rsf, oss, osr, oso
+            self.rss, self.rsr, self.rsf, self.oss, self.osr = rss, rsr, rsf, oss, osr
             self.first, self.width = first, width
 
         def rows(self, q, dx, cc):
@@ -174,13 +174,13 @@
                    self.fm.at[q, 0], self.fp.at[q, 0], self.fm.at[q, 1])[m]
             return remote(src, dst, self.rss, (self.rsr if m < 2 else self.rsf).at[q], dev(dx=1 if m % 2 == 0 else -1))
 
-        def piece(self, q, cx, own=False):
+        def place(self, q):
             n = nb * self.width
             col = (2 * y + c) * nd + (self.first + (q // Y) * self.width) * nb
-            dst = out.at[:, pl.ds(pl.multiple_of(col, nb), n)]
-            if own:
-                return pltpu.make_async_copy(self.s.at[q, cx], dst, self.oso)
-            return remote(self.s.at[q, cx], dst, self.oss, self.osr, dev(cx=cx, dy=lax.rem(q, Y)))
+            return out.at[:, pl.ds(pl.multiple_of(col, nb), n)]
+
+        def piece(self, q, cx):
+            return remote(self.s.at[q, cx], self.place(q), self.oss, self.osr, dev(cx=cx, dy=lax.rem(q, Y)))
 
         def tile(self, q):
             blk = self.first + (q // Y) * self.width
@@ -221,7 +221,7 @@
 
             @pl.when(lax.rem(q, Y) == 0)
             def _():
-                self.piece(q, 0, True).start()
+                self.place(q)[...] = self.s[q, 0]
 
             @pl.when(lax.rem(q, Y) != 0)
             def _():
@@ -230,33 +230,33 @@
         def end(self, tiles):
             left(self.c.at[pl.ds(0, tiles * 6 // (2 * X)), :, :], self.rss)
             left(self.s.at[pl.ds(0, tiles * 7 // 8)], self.oss)
-            landed(self.s.at[pl.ds(0, tiles // 8)], self.oso)
             landed(self.s.at[pl.ds(0, tiles * 7 // 8)], self.osr)
 
-    two = Tiles(c2, rp2, rm2, fp2, fm2, s2_, rss2, rsr2, rsf2, oss2, osr2, oso2, 0, 2)
-    one = Tiles(c1, rp1, rm1, fp1, fm1, s1_, rss1, rsr1, rsf1, oss1, osr1, oso1, 2 * PAIRS, 1)
-
-    for blk in range(BLOCKS):
-        bown(blk).start()
-    aown().start()
+    two = Tiles(c2, rp2, rm2, fp2, fm2, s2_, rss2, rsr2, rsf2, oss2, osr2, 0, 2)
+    one = Tiles(c1, rp1, rm1, fp1, fm1, s1_, rss1, rsr1, rsf1, oss1, osr1, 2 * PAIRS, 1)
 
     peers = [dict(dx=1), dict(dx=2), dict(dx=3), dict(dz=1), dict(dz=-1)]
     peers += [dict(cx=cx, dy=dy) for cx, dy in BP]
     barrier = pltpu.get_barrier_semaphore()
     for p in peers:
         pl.semaphore_signal(barrier, inc=1, device_id=dev(**p), device_id_type=pl.DeviceIdType.MESH)
+    for blk in range(BLOCKS):
+        bown(blk).start()
+    aown().start()
     landed(b_buf.at[:, 0, pl.ds(pl.multiple_of(z * rb, rb), rb), :], bo)
     pl.semaphore_wait(barrier, len(peers))
 
     def a_first():
         ax(1).start()
         ax(3).start()
-        ax(2).start()
-        bstart(0)
-        bstart(1)
+        for blk in range(3):
+            bstart(blk)
         ay(1, 0).start()
         ay(0, 0).start()
         ad(0, 0).start()
+
+    def a_far():
+        ax(2).start()
 
     def a_x(k):
         ax(k).wait_recv()
@@ -300,13 +300,14 @@
                 for fn, *arg in calls:
                     fn(*arg)
 
-    ahead = {0: [(a_first,)], 5: [(a_x, 1), (a_x, 3)], 12: [(a_x, 2), (a_y, 0), (a_y, 1)], 14: [(a_y, 3)],
-             18: [(a_y, 2)]}
-    beside = {FIRST: [(a_rows, 0), (a_rows, 1), (a_rows, 3)], 26: [(a_f, 0), (a_f, 1)], 29: [(a_f, 3), (a_f, 2)],
+    ahead = {0: [(a_first,)], 3: [(a_far,)], 6: [(a_x, 1), (a_x, 3)], 12: [(a_x, 2)], 13: [(a_y, 0), (a_y, 1)], 16: [(a_y, 3)],
+             20: [(a_y, 2)]}
+    beside = {FIRST: [(a_rows, 0), (a_rows, 1), (a_rows, 3)], 27: [(a_f, 0), (a_f, 1)], 30: [(a_f, 3), (a_f, 2)],
               FIRST + 10: [(a_rows, 2)]}
-    tail = {44: [(last_hop, 1, 0, recv), (last_hop, 2, 0, start), (last_hop, 1, 1, recv), (last_hop, 2, 1, start)],
-            47: [(last_hop, 2, 0, recv), (last_hop, 1, 0, sent), (last_hop, 3, 0, start)],
-            50: [(last_hop, 2, 1, recv), (last_hop, 1, 1, sent)], 52: [(last_hop, 3, 0, recv)]}
+    tail = {42: [(last_hop, 1, 0, recv), (last_hop, 2, 0, start)],
+            45: [(last_hop, 1, 1, recv), (last_hop, 2, 1, start)],
+            46: [(last_hop, 2, 0, recv), (last_hop, 1, 0, sent), (last_hop, 3, 0, start)],
+            48: [(last_hop, 2, 1, recv), (last_hop, 1, 1, sent)], 50: [(last_hop, 3, 0, recv)]}
     last_slot = SINGLE + 6 * (BLOCKS - 2 * PAIRS - 1) + Y - 1
 
     def pair_stage(slot, name, lag):
@@ -320,37 +321,42 @@
         def _():
             getattr(two, name)(q)
 
-    def block_stage(slot, name, lag):
+    def block_stage(slot, name, lag, first=0, last=BLOCKS - 2 * PAIRS):
         v = slot - SINGLE - lag
         k, r = v // 6, lax.rem(v, 6)
 
-        @pl.when((v >= 0) & (k < BLOCKS - 2 * PAIRS) & (r < Y))
+        @pl.when((v >= 6 * first) & (k < last) & (r < Y))
         def _():
             getattr(one, name)(Y * k + r)
 
+    def both_stages(slot, name, lag, last_lag):
+        n = BLOCKS - 2 * PAIRS
+        block_stage(slot, name, lag, 0, n - 1)
+        block_stage(slot, name, last_lag, n - 1, n)
+
     def slots(slot, carry):
-        @pl.when(slot < 32 + 16)
+        @pl.when(slot < 32 + 12)
         def _():
             pair_stage(slot, "send", 1)
             pair_stage(slot, "send_relayed", 7)
-            pair_stage(slot, "output", 15)
+            pair_stage(slot, "output", 12)
             pair_stage(slot, "relay", 6)
-            pair_stage(slot, "finish", 14)
+            pair_stage(slot, "finish", 11)
             pair_stage(slot, "tile", 0)
 
         @pl.when(slot >= SINGLE)
         def _():
             block_stage(slot, "send", 1)
 
-            @pl.when((slot >= 44) & (slot <= 52))
+            @pl.when((slot >= 42) & (slot <= 50))
             def _():
                 run(slot, tail)
 
-            block_stage(slot, "send_relayed", 5)
-            block_stage(slot, "output", 10)
+            both_stages(slot, "send_relayed", 6, 5)
+            both_stages(slot, "output", 12, 9)
             block_stage(slot, "tile", 0)
-            block_stage(slot, "relay", 4)
-            block_stage(slot, "finish", 9)
+            both_stages(slot, "relay", 5, 4)
+            both_stages(slot, "finish", 11, 8)
 
         return carry
 
@@ -372,11 +378,14 @@
             @pl.when(t == END - 2)
             def _():
                 last_hop(1, 0, start)
+
+            @pl.when(t == END - 1)
+            def _():
                 last_hop(1, 1, start)
 
-            @pl.when((ahead3 == 1) & (t >= 4) & (t < 3 * BLOCKS - 2))
-            def _():
-                bstart((t + 2) // 3)
+            @pl.when((ahead3 == 1) & (t < 3 * (BLOCKS - 3)))
+            def _():
+                bstart((t + 8) // 3)
 
             @pl.when(t < FIRST)
             def _():
@@ -393,7 +402,7 @@
 
         return carry
 
-    lax.fori_loop(0, FIRST + (last_slot + 10) // 2 + 1, tick, None)
+    lax.fori_loop(0, FIRST + (last_slot + 9) // 2 + 1, tick, None)
 
     def ring_sent(t, carry):
         ring(t, sent)
@@ -431,17 +440,17 @@
             *both(2, ra, dtype=bf16),
             dma((2, 4)), dma((2, 4)), dma((2, 4)), dma((2, 4)),
             dma, dma((BLOCKS,)), dma, dma((X,)), dma((2, X)), dma((X,)), dma((Y,)), dma, dma,
-            dma, dma((PT,)), dma((PT,)), dma, dma, dma,
-            dma, dma((ST,)), dma((ST,)), dma, dma, dma,
+            dma, dma((PT,)), dma((PT,)), dma, dma,
+            dma, dma((ST,)), dma((ST,)), dma, dma,
         ]
         return pl.pallas_call(
             kernel,
-            out_shape=jax.ShapeDtypeStruct((ra, n), bf16),
+            out_shape=pltpu.VMEM((ra, n), bf16),
             in_specs=[pl.BlockSpec(memory_space=pl.ANY)] * 2,
-            out_specs=pl.BlockSpec(memory_space=pl.ANY),
+            out_specs=pl.BlockSpec(memory_space=pltpu.VMEM),
             scratch_shapes=scratch,
             compiler_params=pltpu.CompilerParams(
-                collective_id=0, has_side_effects=True, vmem_limit_bytes=67043328),
+                collective_id=0, has_side_effects=True, vmem_limit_bytes=62000000),
         )(a_rows, b_rows)
 
     return jax.shard_map(device_block, mesh=mesh, in_specs=(P(all_axes, None), P(all_axes, None)),

time: 217 us -> 211 us (0.972)
  Pallas kernels: 215 us -> 210 us
    pallas_call x1, Pallas kernels: 215 us -> 210 us  [device_block(): pl.pallas_call(kernel, out_shape=pltpu.VMEM((ra, n), bf16), in_specs=[pl....]
where the time goes in v4:
time: 211 us
  Pallas kernels  210 us (100%)
    pallas_call x1, Pallas kernels, device_block(): pl.pallas_call(kernel, out_shape=pltpu.VMEM((ra, n), bf16), in_specs=[pl....  210 us

profile of v4, /device:TPU:1, one launch (start us, length us, event | category | flops | bytes accessed | tf_op | source)
XLA Modules:
  0.0 210.9 jit_solution(1720988551245012503)
XLA Ops:
  0.0 209.8 %shard_map.28 = bf16[48,12288]{1,0:T(8,128)(2,1)S(1)} custom-call(bf16[48,24576]{1,0:T(8,128)(2,1)} %a_in.1, bf16[96,12288]{1,0:T(8,128)(2,1)} %b_in.1), custom_call_target="tpu_custom_call" | custom-call | tf_op jit(solution)/shard_map/pallas_call | solution.py:446
  209.8 1.0 copy.4

commit v5 on v4

--- a/solution.py
+++ b/solution.py
@@ -300,7 +300,7 @@
                 for fn, *arg in calls:
                     fn(*arg)
 
-    ahead = {0: [(a_first,)], 3: [(a_far,)], 6: [(a_x, 1), (a_x, 3)], 12: [(a_x, 2)], 13: [(a_y, 0), (a_y, 1)], 16: [(a_y, 3)],
+    ahead = {0: [(a_first,)], 3: [(a_far,)], 7: [(a_x, 3)], 8: [(a_x, 1)], 12: [(a_x, 2)], 13: [(a_y, 0)], 14: [(a_y, 3)], 17: [(a_y, 1)],
              20: [(a_y, 2)]}
     beside = {FIRST: [(a_rows, 0), (a_rows, 1), (a_rows, 3)], 27: [(a_f, 0), (a_f, 1)], 30: [(a_f, 3), (a_f, 2)],
               FIRST + 10: [(a_rows, 2)]}

time: 211 us -> 210 us (level)
  no operation moved by 1% of the time
where the time goes in v5:
time: 210 us
  Pallas kernels  209 us (100%)
    pallas_call x1, Pallas kernels, device_block(): pl.pallas_call(kernel, out_shape=pltpu.VMEM((ra, n), bf16), in_specs=[pl....  209 us

profile of v5, /device:TPU:1, one launch (start us, length us, event | category | flops | bytes accessed | tf_op | source)
XLA Modules:
  0.0 209.6 jit_solution(7481765951712549150)
XLA Ops:
  0.0 208.6 %shard_map.28 = bf16[48,12288]{1,0:T(8,128)(2,1)S(1)} custom-call(bf16[48,24576]{1,0:T(8,128)(2,1)} %a_in.1, bf16[96,12288]{1,0:T(8,128)(2,1)} %b_in.1), custom_call_target="tpu_custom_call" | custom-call | tf_op jit(solution)/shard_map/pallas_call | solution.py:446
  208.6 1.0 copy.4

commit v6 on v5

--- a/solution.py
+++ b/solution.py
@@ -327,7 +327,7 @@
 
         @pl.when((v >= 6 * first) & (k < last) & (r < Y))
         def _():
-            getattr(one, name)(Y * k + r)
+            getattr(one, name)(Y * k + Y - 1 - r)
 
     def both_stages(slot, name, lag, last_lag):
         n = BLOCKS - 2 * PAIRS
@@ -352,10 +352,10 @@
             def _():
                 run(slot, tail)
 
-            both_stages(slot, "send_relayed", 6, 5)
+            both_stages(slot, "send_relayed", 5, 5)
             both_stages(slot, "output", 12, 9)
             block_stage(slot, "tile", 0)
-            both_stages(slot, "relay", 5, 4)
+            both_stages(slot, "relay", 4, 4)
             both_stages(slot, "finish", 11, 8)
 
         return carry

time: 210 us -> 209 us (level)
  no operation moved by 1% of the time
where the time goes in v6:
time: 209 us
  Pallas kernels  208 us (100%)
    pallas_call x1, Pallas kernels, device_block(): pl.pallas_call(kernel, out_shape=pltpu.VMEM((ra, n), bf16), in_specs=[pl....  208 us

profile of v6, /device:TPU:1, one launch (start us, length us, event | category | flops | bytes accessed | tf_op | source)
XLA Modules:
  0.0 209.2 jit_solution(257778490021202352)
XLA Ops:
  0.0 208.2 %shard_map.28 = bf16[48,12288]{1,0:T(8,128)(2,1)S(1)} custom-call(bf16[48,24576]{1,0:T(8,128)(2,1)} %a_in.1, bf16[96,12288]{1,0:T(8,128)(2,1)} %b_in.1), custom_call_target="tpu_custom_call" | custom-call | tf_op jit(solution)/shard_map/pallas_call | solution.py:446
  208.2 1.0 copy.4
